TPU v7x, 32 devices: a whole 2x2x4 slice. The times are simulated.
32 devices in a mesh: row: 8 (over z, y), col: 4 (over x, core).
Axes of the slice: x: 2, y: 2, z: 4, core: 2. Of those that a mesh axis runs over, the one named last changes fastest.
Arguments:
- right_side: float32 [3, 64, 512], P(None, 'row', 'col'), may hold values from -6 to 6
- viscosity: float32 [64, 512], P('row', 'col'), may hold values from 0.1 to 3
- free_mask: int32 [3, 64, 512], P(None, 'row', 'col'), may hold values 0 or 1
- coarse_basis: float32 [64, 3, 64, 512], P(None, None, 'row', 'col'), may hold values from -6 to 6
- gram_inverse: float32 [64, 64], P('col'), may hold values from -3 to 6, as said below
Outputs:
- solution: float32 [3, 64, 512], P(None, 'row', 'col')
- residual: float32 [3, 64, 512], P(None, 'row', 'col')
Inputs may be any that keep to these rules, and one draw needn't show every extreme that they name: `free_mask`: 1 marks a free velocity unknown, 0 one whose value is prescribed. `gram_inverse`: symmetric positive definite.
All inputs are finite; a program needn't handle non-finite values. No bound on the sum of `free_mask` on one device may be relied on, other than what follows from the above.
Results may differ from a plain program's by a relative error of at most 0.0003.
Values sent between devices are 32-bit elements; how exact they have to be, the bound alone decides.
A program may use at most 64 MiB of HBM per device.

v0:
```python
import math
import jax
import jax.numpy as jnp
from jax import lax
from jax.sharding import PartitionSpec as P

ITERS = 2


def padded_2(shard, sides, width):
    for axis, dim in sides:
        count, length = (lax.axis_size(axis), shard.shape[dim])
        up = [(i, (i + 1) % count) for i in range(count - 1)]
        down = [(j, i) for i, j in up]
        last = lax.slice_in_dim(shard, length - width, length, axis=dim)
        leading = lax.slice_in_dim(shard, 0, width, axis=dim)
        before = lax.ppermute(last, axis, up)
        after = lax.ppermute(leading, axis, down)
        shard = jnp.concatenate([before, shard, after], axis=dim)
    return shard


def on_device(right_side, viscosity, free_mask, coarse_basis, gram_inverse):
    high = lax.Precision.HIGHEST
    components, patch_rows, patch_cols = right_side.shape
    columns = coarse_basis.shape[0]
    unknowns = (
        components * patch_rows * patch_cols * lax.axis_size("row") * lax.axis_size("col") * columns
    )
    coarse_scale = 1.0 / (32.0 * math.sqrt(float(unknowns)))
    viscosity_pad = padded_2(viscosity, (("row", 0), ("col", 1)), 1)
    face_north = 0.5 * (viscosity + viscosity_pad[2:, 1:-1])
    face_south = 0.5 * (viscosity + viscosity_pad[:-2, 1:-1])
    face_east = 0.5 * (viscosity + viscosity_pad[1:-1, 2:])
    face_west = 0.5 * (viscosity + viscosity_pad[1:-1, :-2])
    diagonal = 1.0 + face_north + face_south + face_east + face_west
    unfixed = free_mask.astype(jnp.float32)
    jacobi = unfixed / diagonal + (1.0 - unfixed)
    basis_rows = coarse_basis.reshape(columns, -1)

    def solve_coarse(coarse_dot):
        coeff_part = jnp.dot(gram_inverse, coarse_dot, precision=high) * coarse_scale
        return lax.all_gather(coeff_part, "col", axis=0, tiled=True)

    def precondition(residual, coarse_dot, weighted_sq):
        coeffs = solve_coarse(coarse_dot)
        smoothed = jacobi * residual + jnp.dot(coeffs, basis_rows, precision=high).reshape(
            residual.shape
        )
        return (smoothed, weighted_sq + jnp.dot(coarse_dot, coeffs, precision=high))

    solution = jnp.zeros_like(right_side)
    residual = right_side
    coarse_dot, weighted_sq = lax.psum(
        (
            jnp.dot(basis_rows, residual.reshape(-1), precision=high),
            jnp.sum(jacobi * residual * residual),
        ),
        ("row", "col"),
    )
    direction, energy = precondition(residual, coarse_dot, weighted_sq)
    for iteration in range(ITERS):
        masked = unfixed * direction
        padded = padded_2(masked, (("row", 1), ("col", 2)), 1)
        stencil = diagonal * masked - (
            face_north * padded[:, 2:, 1:-1]
            + face_south * padded[:, :-2, 1:-1]
            + face_east * padded[:, 1:-1, 2:]
            + face_west * padded[:, 1:-1, :-2]
        )
        applied = unfixed * stencil + (1.0 - unfixed) * direction
        if iteration + 1 < ITERS:
            curve_sum, image_coarse, cross_term, image_sq = lax.psum(
                (
                    jnp.sum(direction * applied),
                    jnp.dot(basis_rows, applied.reshape(-1), precision=high),
                    jnp.sum(jacobi * residual * applied),
                    jnp.sum(jacobi * applied * applied),
                ),
                ("row", "col"),
            )
            step_len = energy / curve_sum
            solution = step_len * direction
            residual = residual - step_len * applied
            coarse_dot = coarse_dot - step_len * image_coarse
            weighted_sq = weighted_sq - 2.0 * step_len * cross_term + step_len * step_len * image_sq
            smoothed, energy_new = precondition(residual, coarse_dot, weighted_sq)
            direction = smoothed + energy_new / energy * direction
            energy = energy_new
        else:
            curve_sum = lax.psum(jnp.sum(direction * applied), ("row", "col"))
            step_len = energy / curve_sum
            solution = solution + step_len * direction
            residual = residual - step_len * applied
    return (solution, residual)


def solution(mesh):
    in_specs = (
        P(None, "row", "col"),
        P("row", "col"),
        P(None, "row", "col"),
        P(None, None, "row", "col"),
        P("col", None),
    )
    out_specs = (P(None, "row", "col"), P(None, "row", "col"))
    return jax.shard_map(
        on_device, mesh=mesh, in_specs=in_specs, out_specs=out_specs, check_vma=False
    )
```

profile of v0, /device:TPU:0, one launch (start us, length us, event | category | flops | bytes accessed | tf_op | source)
XLA Modules:
  0.0 198.3 jit_solution(4688476039508117926)
XLA Ops:
  1.4 1.3 collective-permute-start
  2.7 5.5 %collective-permute-start.1 = (f32[1,128]{1,0:T(1,128)S(1)}, f32[1,128]{1,0:T(1,128)S(1)}, u32[]{:S(2)}, u32[]{:S(2)}) collective-permute-start(f32[1,128]{1,0:T(1,128)S(1)} %get-tuple-element.33), channel_id=1, source_target_pairs={{0,4},{4,8},{8,12},{12,16},{16,20},{20,24},{24,28},{1,5},{5,9},{9,... | collective-permute-start | bytes 1544 | tf_op jit(solution)/shard_map/ppermute | solution.py:17
  8.2 1.3 copy.32
  9.7 1.0 copy-done.1
  11.4 41.9 %psum.50 = f32[64]{0:T(128)S(1)} all-reduce(f32[64]{0:T(128)S(1)} %convolution_bitcast_fusion.3), channel_id=1, replica_groups=mesh['row'=8,'col'=4] {'row','col'}, use_global_device_ids=true, to_apply=%region_2.0 | all-reduce | flops 64 | bytes 512 | tf_op jit(solution)/shard_map/psum | solution.py:54
  55.5 5.8 %all-reduce = f32[64]{0:T(128)S(1)} all-reduce(f32[64]{0:T(128)S(1)} %dynamic-update-slice), channel_id=1, replica_groups=mesh['row'=8,'col'=4] {'col'}, use_global_device_ids=true, to_apply=%add | all-reduce | flops 64 | bytes 512
  62.1 1.3 collective-permute-start.2
  63.4 3.0 %collective-permute-start.3 = (f32[10,1]{1,0:T(8,128)S(1)}, f32[10,1]{1,0:T(8,128)S(1)}, u32[]{:S(2)}, u32[]{:S(2)}) collective-permute-start(f32[10,1]{1,0:T(8,128)S(1)} %get-tuple-element.31), channel_id=1, source_target_pairs={{0,1},{1,2},{2,3},{4,5},{5,6},{6,7},{8,9},{9,10},{10,11},{12,13},{... | collective-permute-start | bytes 128 | tf_op jit(solution)/shard_map/ppermute | solution.py:17
  66.5 0.8 collective-permute-done.3
  67.4 1.3 collective-permute-start.4
  68.7 4.8 %collective-permute-start.5 = (f32[3,1,128]{2,1,0:T(1,128)S(1)}, f32[3,1,128]{2,1,0:T(1,128)S(1)}, u32[]{:S(2)}, u32[]{:S(2)}) collective-permute-start(f32[3,1,128]{2,1,0:T(1,128)S(1)} %get-tuple-element.29), channel_id=1, source_target_pairs={{0,4},{4,8},{8,12},{12,16},{16,20},{20,24},{24,28},{1,5},{5,9},{9,... | collective-permute-start | bytes 4616 | tf_op jit(solution)/shard_map/ppermute | solution.py:17
  73.5 1.3 collective-permute-done.5
  74.9 2.3 %collective-permute-start.7 = (f32[3,10,1]{2,1,0:T(8,128)S(1)}, f32[3,10,1]{2,1,0:T(8,128)S(1)}, u32[]{:S(2)}, u32[]{:S(2)}) collective-permute-start(f32[3,10,1]{2,1,0:T(8,128)S(1)} %get-tuple-element.26), channel_id=1, source_target_pairs={{0,1},{1,2},{2,3},{4,5},{5,6},{6,7},{8,9},{9,10},{10,11},{12,13},{... | collective-permute-start | bytes 368 | tf_op jit(solution)/shard_map/ppermute | solution.py:17
  77.2 1.3 collective-permute-start.6
  79.1 4.0 %collective-permute-done.6 = f32[3,10,1]{2,1,0:T(8,128)S(1)} collective-permute-done((f32[3,10,1]{2,1,0:T(8,128)S(1)}, f32[3,10,1]{2,1,0:T(8,128)S(1)}, u32[]{:S(2)}, u32[]{:S(2)}) %collective-permute-start.6) | collective-permute-done | bytes 152 | tf_op jit(solution)/shard_map/ppermute | solution.py:18
  84.6 42.6 %all-reduce.2 = (f32[64]{0:T(128)S(1)}, f32[]{:T(128)}, f32[]{:T(128)}, f32[]{:T(128)}, f32[]{:T(128)}) all-reduce(f32[64]{0:T(128)S(1)} %convolution_bitcast_fusion.1, f32[]{:T(128)} %get-tuple-element.4, f32[]{:T(128)} %get-tuple-element.5, f32[]{:T(128)} %get-tuple-element.3, ...), channel_id=1, replica_groups=mesh['row'=8,'col'=4] {'row','col'}, use_global_device_ids=true, to_apply=%region_9.0 | all-reduce | flops 68 | bytes 544 | tf_op jit(solution)/shard_map/psum | solution.py:73
  129.5 7.6 %all-reduce.1 = f32[64]{0:T(128)S(1)} all-reduce(f32[64]{0:T(128)S(1)} %dynamic-update-slice.1), channel_id=1, replica_groups=mesh['row'=8,'col'=4] {'col'}, use_global_device_ids=true, to_apply=%add.1 | all-reduce | flops 64 | bytes 512
  140.8 1.3 collective-permute-start.8
  142.1 4.5 %collective-permute-start.9 = (f32[3,1,128]{2,1,0:T(1,128)S(1)}, f32[3,1,128]{2,1,0:T(1,128)S(1)}, u32[]{:S(2)}, u32[]{:S(2)}) collective-permute-start(f32[3,1,128]{2,1,0:T(1,128)S(1)} %get-tuple-element.27), channel_id=1, source_target_pairs={{0,4},{4,8},{8,12},{12,16},{16,20},{20,24},{24,28},{1,5},{5,9},{9,... | collective-permute-start | bytes 4616 | tf_op jit(solution)/shard_map/ppermute | solution.py:17
  146.7 1.3 collective-permute-done.9
  148.0 1.3 collective-permute-start.11
  149.3 1.3 collective-permute-start.10
  150.6 2.6 %collective-permute-done.10 = f32[3,10,1]{2,1,0:T(8,128)S(1)} collective-permute-done((f32[3,10,1]{2,1,0:T(8,128)S(1)}, f32[3,10,1]{2,1,0:T(8,128)S(1)}, u32[]{:S(2)}, u32[]{:S(2)}) %collective-permute-start.10) | collective-permute-done | bytes 152 | tf_op jit(solution)/shard_map/ppermute | solution.py:18
  154.0 43.0 %psum.55 = f32[]{:T(128)} all-reduce(f32[]{:T(128)} %get-tuple-element.11), channel_id=1, replica_groups=mesh['row'=8,'col'=4] {'row','col'}, use_global_device_ids=true, to_apply=%region_11.0 | all-reduce | flops 1 | bytes 8 | tf_op jit(solution)/shard_map/psum | solution.py:91
  (47 shorter events, 9.3 us)
Async XLA Ops:
  0.6 52.6 %copy-start = (f32[16,64]{1,0:T(8,128)S(1)}, f32[16,64]{1,0:T(8,128)}, u32[]{:S(2)}) copy-start(f32[16,64]{1,0:T(8,128)} %param.9) | copy-start | bytes 12292
  1.4 60.5 %collective-permute-start = (f32[1,128]{1,0:T(1,128)S(1)}, f32[1,128]{1,0:T(1,128)S(1)}, u32[]{:S(2)}, u32[]{:S(2)}) collective-permute-start(f32[1,128]{1,0:T(1,128)S(1)} %get-tuple-element.34), channel_id=1, source_target_pairs={{4,0},{8,4},{12,8},{16,12},{20,16},{24,20},{28,24},{5,1},{9,5},{13... | collective-permute-start | bytes 1544 | tf_op jit(solution)/shard_map/ppermute | solution.py:18
  2.7 59.2 %collective-permute-start.1 = (f32[1,128]{1,0:T(1,128)S(1)}, f32[1,128]{1,0:T(1,128)S(1)}, u32[]{:S(2)}, u32[]{:S(2)}) collective-permute-start(f32[1,128]{1,0:T(1,128)S(1)} %get-tuple-element.33), channel_id=1, source_target_pairs={{0,4},{4,8},{8,12},{12,16},{16,20},{20,24},{24,28},{1,5},{5,9},{9,... | collective-permute-start | bytes 1544 | tf_op jit(solution)/shard_map/ppermute | solution.py:17
  9.5 1.1 copy-start.1
  9.5 1.1 copy-start.2
  53.4 0.7 copy-start.5
  61.3 0.7 copy-start.4
  62.0 5.3 %copy-start.3 = (s32[3,8,128]{2,1,0:T(8,128)S(1)}, s32[3,8,128]{2,1,0:T(8,128)}, u32[]{:S(2)}) copy-start(s32[3,8,128]{2,1,0:T(8,128)} %param.7) | copy-start | bytes 36868
  62.1 4.3 %collective-permute-start.2 = (f32[10,1]{1,0:T(8,128)S(1)}, f32[10,1]{1,0:T(8,128)S(1)}, u32[]{:S(2)}, u32[]{:S(2)}) collective-permute-start(f32[10,1]{1,0:T(8,128)S(1)} %get-tuple-element.32), channel_id=1, source_target_pairs={{1,0},{2,1},{3,2},{5,4},{6,5},{7,6},{9,8},{10,9},{11,10},{13,12},{... | collective-permute-start | bytes 128 | tf_op jit(solution)/shard_map/ppermute | solution.py:18
  63.4 3.8 %collective-permute-start.3 = (f32[10,1]{1,0:T(8,128)S(1)}, f32[10,1]{1,0:T(8,128)S(1)}, u32[]{:S(2)}, u32[]{:S(2)}) collective-permute-start(f32[10,1]{1,0:T(8,128)S(1)} %get-tuple-element.31), channel_id=1, source_target_pairs={{0,1},{1,2},{2,3},{4,5},{5,6},{6,7},{8,9},{9,10},{10,11},{12,13},{... | collective-permute-start | bytes 128 | tf_op jit(solution)/shard_map/ppermute | solution.py:17
  67.4 6.1 %collective-permute-start.4 = (f32[3,1,128]{2,1,0:T(1,128)S(1)}, f32[3,1,128]{2,1,0:T(1,128)S(1)}, u32[]{:S(2)}, u32[]{:S(2)}) collective-permute-start(f32[3,1,128]{2,1,0:T(1,128)S(1)} %get-tuple-element.30), channel_id=1, source_target_pairs={{4,0},{8,4},{12,8},{16,12},{20,16},{24,20},{28,24},{5,1},{9,5},{13... | collective-permute-start | bytes 4616 | tf_op jit(solution)/shard_map/ppermute | solution.py:18
  68.7 6.1 %collective-permute-start.5 = (f32[3,1,128]{2,1,0:T(1,128)S(1)}, f32[3,1,128]{2,1,0:T(1,128)S(1)}, u32[]{:S(2)}, u32[]{:S(2)}) collective-permute-start(f32[3,1,128]{2,1,0:T(1,128)S(1)} %get-tuple-element.29), channel_id=1, source_target_pairs={{0,4},{4,8},{8,12},{12,16},{16,20},{20,24},{24,28},{1,5},{5,9},{9,... | collective-permute-start | bytes 4616 | tf_op jit(solution)/shard_map/ppermute | solution.py:17
  74.9 4.3 %collective-permute-start.7 = (f32[3,10,1]{2,1,0:T(8,128)S(1)}, f32[3,10,1]{2,1,0:T(8,128)S(1)}, u32[]{:S(2)}, u32[]{:S(2)}) collective-permute-start(f32[3,10,1]{2,1,0:T(8,128)S(1)} %get-tuple-element.26), channel_id=1, source_target_pairs={{0,1},{1,2},{2,3},{4,5},{5,6},{6,7},{8,9},{9,10},{10,11},{12,13},{... | collective-permute-start | bytes 368 | tf_op jit(solution)/shard_map/ppermute | solution.py:17
  77.2 6.0 %collective-permute-start.6 = (f32[3,10,1]{2,1,0:T(8,128)S(1)}, f32[3,10,1]{2,1,0:T(8,128)S(1)}, u32[]{:S(2)}, u32[]{:S(2)}) collective-permute-start(f32[3,10,1]{2,1,0:T(8,128)S(1)} %get-tuple-element.25), channel_id=1, source_target_pairs={{1,0},{2,1},{3,2},{5,4},{6,5},{7,6},{9,8},{10,9},{11,10},{13,12},{... | collective-permute-start | bytes 368 | tf_op jit(solution)/shard_map/ppermute | solution.py:18
  140.8 5.9 %collective-permute-start.8 = (f32[3,1,128]{2,1,0:T(1,128)S(1)}, f32[3,1,128]{2,1,0:T(1,128)S(1)}, u32[]{:S(2)}, u32[]{:S(2)}) collective-permute-start(f32[3,1,128]{2,1,0:T(1,128)S(1)} %get-tuple-element.28), channel_id=1, source_target_pairs={{4,0},{8,4},{12,8},{16,12},{20,16},{24,20},{28,24},{5,1},{9,5},{13... | collective-permute-start | bytes 4616 | tf_op jit(solution)/shard_map/ppermute | solution.py:18
  142.1 5.8 %collective-permute-start.9 = (f32[3,1,128]{2,1,0:T(1,128)S(1)}, f32[3,1,128]{2,1,0:T(1,128)S(1)}, u32[]{:S(2)}, u32[]{:S(2)}) collective-permute-start(f32[3,1,128]{2,1,0:T(1,128)S(1)} %get-tuple-element.27), channel_id=1, source_target_pairs={{0,4},{4,8},{8,12},{12,16},{16,20},{20,24},{24,28},{1,5},{5,9},{9,... | collective-permute-start | bytes 4616 | tf_op jit(solution)/shard_map/ppermute | solution.py:17
  148.0 2.6 %collective-permute-start.11 = (f32[3,10,1]{2,1,0:T(8,128)S(1)}, f32[3,10,1]{2,1,0:T(8,128)S(1)}, u32[]{:S(2)}, u32[]{:S(2)}) collective-permute-start(f32[3,10,1]{2,1,0:T(8,128)S(1)} %get-tuple-element.24), channel_id=1, source_target_pairs={{0,1},{1,2},{2,3},{4,5},{5,6},{6,7},{8,9},{9,10},{10,11},{12,13},{... | collective-permute-start | bytes 368 | tf_op jit(solution)/shard_map/ppermute | solution.py:17
  149.3 3.9 %collective-permute-start.10 = (f32[3,10,1]{2,1,0:T(8,128)S(1)}, f32[3,10,1]{2,1,0:T(8,128)S(1)}, u32[]{:S(2)}, u32[]{:S(2)}) collective-permute-start(f32[3,10,1]{2,1,0:T(8,128)S(1)} %get-tuple-element.23), channel_id=1, source_target_pairs={{1,0},{2,1},{3,2},{5,4},{6,5},{7,6},{9,8},{10,9},{11,10},{13,12},{... | collective-permute-start | bytes 368 | tf_op jit(solution)/shard_map/ppermute | solution.py:18
where the time goes:
time: 199 us; the launch traced here: 198 us
  blocking collectives  141 us (71%)
  starting transfers between devices  29.2 us (15%)
  waiting for transfers between devices  10 us (5%)
  between operations  6.67 us (3%)
  local copies, waits for them, and re-layouts  5.22 us (3%)
  other arithmetic  3.45 us (2%)
  matrix products  2.83 us (1%)
    psum x1, blocking collectives, on_device(): curve_sum = lax.psum(jnp.sum(direction * applied), ('row', 'col'))  43 us
    psum x1, blocking collectives, on_device(): lax.psum((jnp.sum(direction * applied), jnp.dot(basis_rows, applied.resha...  42.6 us
    psum x1, blocking collectives, on_device(): lax.psum((jnp.dot(basis_rows, residual.reshape(-1), precision=high), jnp....  41.9 us
    ppermute x6, starting transfers between devices, padded_2(): before = lax.ppermute(last, axis, up)  21.5 us
    unnamed x2, blocking collectives  13.4 us
    ppermute x6, starting transfers between devices, padded_2(): after = lax.ppermute(leading, axis, down)  7.73 us
    ppermute x6, waiting for transfers between devices, padded_2(): after = lax.ppermute(leading, axis, down)  6.67 us
    unnamed x19, local copies, waits for them, and re-layouts  4.22 us
  transfers between devices with their start and end apart: 12, of which 5 were waited for; matrix products, arithmetic and copies ran while one was open for 2% of the time, Pallas kernels for 0%

commit v1 on v0

--- a/solution.py
+++ b/solution.py
@@ -3,6 +3,7 @@
 import jax.numpy as jnp
 from jax import lax
 from jax.sharding import PartitionSpec as P
+from jax.lax import psum
 
 ITERS = 2
 
@@ -70,14 +71,19 @@
         )
         applied = unfixed * stencil + (1.0 - unfixed) * direction
         if iteration + 1 < ITERS:
-            curve_sum, image_coarse, cross_term, image_sq = lax.psum(
+
+            def guide_ranges(vals):
+                for src_i in ("col", "row"):
+                    vals = psum(vals, src_i)
+                return vals
+
+            curve_sum, image_coarse, cross_term, image_sq = guide_ranges(
                 (
                     jnp.sum(direction * applied),
                     jnp.dot(basis_rows, applied.reshape(-1), precision=high),
                     jnp.sum(jacobi * residual * applied),
                     jnp.sum(jacobi * applied * applied),
-                ),
-                ("row", "col"),
+                )
             )
             step_len = energy / curve_sum
             solution = step_len * direction

time: 199 us -> 224 us (1.13)
  blocking collectives: 141 us -> 164 us
    psum x1 -> x2, blocking collectives: 41.9 us -> 84.3 us  [on_device(): lax.psum((jnp.dot(basis_rows, residual.reshape(-1), precision=high), jnp....]
    psum x1 -> x2, blocking collectives: 42.6 us -> 27.6 us  [guide_ranges(): vals = psum(vals, src_i)]
    psum x1, blocking collectives: 43 us -> 40.2 us  [on_device(): curve_sum = lax.psum(jnp.sum(direction * applied), ('row', 'col'))]
where the time goes in v1:
time: 224 us; the launch traced here: 223 us
  blocking collectives  164 us (73%)
  starting transfers between devices  29.2 us (13%)
  waiting for transfers between devices  11.6 us (5%)
  between operations  6.82 us (3%)
  local copies, waits for them, and re-layouts  5.22 us (2%)
  other arithmetic  3.44 us (2%)
  matrix products  2.83 us (1%)
    psum x2, blocking collectives, on_device(): lax.psum((jnp.dot(basis_rows, residual.reshape(-1), precision=high), jnp....  84.3 us
    psum x1, blocking collectives, on_device(): curve_sum = lax.psum(jnp.sum(direction * applied), ('row', 'col'))  40.2 us
    psum x2, blocking collectives, guide_ranges(): vals = psum(vals, src_i)  27.6 us
    ppermute x6, starting transfers between devices, padded_2(): before = lax.ppermute(last, axis, up)  21.5 us
    unnamed x2, blocking collectives  11.4 us
    ppermute x6, waiting for transfers between devices, padded_2(): after = lax.ppermute(leading, axis, down)  8.27 us
    ppermute x6, starting transfers between devices, padded_2(): after = lax.ppermute(leading, axis, down)  7.73 us
  transfers between devices with their start and end apart: 12, of which 5 were waited for; matrix products, arithmetic and copies ran while one was open for 2% of the time, Pallas kernels for 0%

profile of v1, /device:TPU:0, one launch (start us, length us, event | category | flops | bytes accessed | tf_op | source)
XLA Modules:
  0.0 222.7 jit_solution(1747593718300653777)
XLA Ops:
  1.4 1.3 collective-permute-start
  2.7 5.5 %collective-permute-start.1 = (f32[1,128]{1,0:T(1,128)S(1)}, f32[1,128]{1,0:T(1,128)S(1)}, u32[]{:S(2)}, u32[]{:S(2)}) collective-permute-start(f32[1,128]{1,0:T(1,128)S(1)} %get-tuple-element.36), channel_id=1, source_target_pairs={{0,4},{4,8},{8,12},{12,16},{16,20},{20,24},{24,28},{1,5},{5,9},{9,... | collective-permute-start | bytes 1544 | tf_op jit(solution)/shard_map/ppermute | solution.py:18
  8.2 1.3 copy.32
  11.4 41.9 %psum.78 = f32[64]{0:T(128)S(1)} all-reduce(f32[64]{0:T(128)S(1)} %convolution_bitcast_fusion.3), channel_id=1, replica_groups=mesh['row'=8,'col'=4] {'row','col'}, use_global_device_ids=true, to_apply=%region_2.0 | all-reduce | flops 64 | bytes 512 | tf_op jit(solution)/shard_map/psum | solution.py:55
  55.5 5.8 %all-reduce = f32[64]{0:T(128)S(1)} all-reduce(f32[64]{0:T(128)S(1)} %dynamic-update-slice), channel_id=1, replica_groups=mesh['row'=8,'col'=4] {'col'}, use_global_device_ids=true, to_apply=%add | all-reduce | flops 64 | bytes 512
  62.1 1.3 collective-permute-start.2
  63.4 3.0 %collective-permute-start.3 = (f32[10,1]{1,0:T(8,128)S(1)}, f32[10,1]{1,0:T(8,128)S(1)}, u32[]{:S(2)}, u32[]{:S(2)}) collective-permute-start(f32[10,1]{1,0:T(8,128)S(1)} %get-tuple-element.34), channel_id=1, source_target_pairs={{0,1},{1,2},{2,3},{4,5},{5,6},{6,7},{8,9},{9,10},{10,11},{12,13},{... | collective-permute-start | bytes 128 | tf_op jit(solution)/shard_map/ppermute | solution.py:18
  67.4 1.3 collective-permute-start.4
  68.7 4.8 %collective-permute-start.5 = (f32[3,1,128]{2,1,0:T(1,128)S(1)}, f32[3,1,128]{2,1,0:T(1,128)S(1)}, u32[]{:S(2)}, u32[]{:S(2)}) collective-permute-start(f32[3,1,128]{2,1,0:T(1,128)S(1)} %get-tuple-element.32), channel_id=1, source_target_pairs={{0,4},{4,8},{8,12},{12,16},{16,20},{20,24},{24,28},{1,5},{5,9},{9,... | collective-permute-start | bytes 4616 | tf_op jit(solution)/shard_map/ppermute | solution.py:18
  73.5 1.3 collective-permute-done.5
  74.9 2.3 %collective-permute-start.7 = (f32[3,10,1]{2,1,0:T(8,128)S(1)}, f32[3,10,1]{2,1,0:T(8,128)S(1)}, u32[]{:S(2)}, u32[]{:S(2)}) collective-permute-start(f32[3,10,1]{2,1,0:T(8,128)S(1)} %get-tuple-element.29), channel_id=1, source_target_pairs={{0,1},{1,2},{2,3},{4,5},{5,6},{6,7},{8,9},{9,10},{10,11},{12,13},{... | collective-permute-start | bytes 368 | tf_op jit(solution)/shard_map/ppermute | solution.py:18
  77.2 1.3 collective-permute-start.6
  79.1 4.0 %collective-permute-done.6 = f32[3,10,1]{2,1,0:T(8,128)S(1)} collective-permute-done((f32[3,10,1]{2,1,0:T(8,128)S(1)}, f32[3,10,1]{2,1,0:T(8,128)S(1)}, u32[]{:S(2)}, u32[]{:S(2)}) %collective-permute-start.6) | collective-permute-done | bytes 152 | tf_op jit(solution)/shard_map/ppermute | solution.py:19
  83.9 42.4 %psum.77 = f32[]{:T(128)} all-reduce(f32[]{:T(128)} %get-tuple-element.4), channel_id=1, replica_groups=mesh['row'=8,'col'=4] {'row','col'}, use_global_device_ids=true, to_apply=%region_1.0 | all-reduce | flops 1 | bytes 8 | tf_op jit(solution)/shard_map/psum | solution.py:55
  128.4 8.4 %all-reduce.3 = (f32[64]{0:T(128)S(1)}, f32[]{:T(128)}, f32[]{:T(128)}, f32[]{:T(128)}) all-reduce(f32[64]{0:T(128)S(1)} %convolution_bitcast_fusion.1, f32[]{:T(128)} %get-tuple-element.5, f32[]{:T(128)} %get-tuple-element.3, f32[]{:T(128)} %get-tuple-element.2), channel_id=1, replica_groups=mesh['row'=8,'col'=4] {'col'}, use_global_device_ids=true, to_apply=%region_12.0 | all-reduce | flops 67 | bytes 536 | tf_op jit(solution)/shard_map/psum | solution.py:77
  136.8 19.3 %all-reduce.2 = (f32[64]{0:T(128)S(1)}, f32[]{:T(128)}, f32[]{:T(128)}, f32[]{:T(128)}) all-reduce(f32[64]{0:T(128)S(1)} %get-tuple-element.10, f32[]{:T(128)} %get-tuple-element.11, f32[]{:T(128)} %get-tuple-element.12, f32[]{:T(128)} %get-tuple-element.13), channel_id=1, replica_groups=mesh['row'=8,'col'=4] {'row'}, use_global_device_ids=true, to_apply=%region_13.0 | all-reduce | flops 67 | bytes 536 | tf_op jit(solution)/shard_map/psum | solution.py:77
  157.0 5.6 %all-reduce.1 = f32[64]{0:T(128)S(1)} all-reduce(f32[64]{0:T(128)S(1)} %dynamic-update-slice.1), channel_id=1, replica_groups=mesh['row'=8,'col'=4] {'col'}, use_global_device_ids=true, to_apply=%add.1 | all-reduce | flops 64 | bytes 512
  166.5 1.3 collective-permute-start.8
  167.8 4.5 %collective-permute-start.9 = (f32[3,1,128]{2,1,0:T(1,128)S(1)}, f32[3,1,128]{2,1,0:T(1,128)S(1)}, u32[]{:S(2)}, u32[]{:S(2)}) collective-permute-start(f32[3,1,128]{2,1,0:T(1,128)S(1)} %get-tuple-element.30), channel_id=1, source_target_pairs={{0,4},{4,8},{8,12},{12,16},{16,20},{20,24},{24,28},{1,5},{5,9},{9,... | collective-permute-start | bytes 4616 | tf_op jit(solution)/shard_map/ppermute | solution.py:18
  172.4 1.3 collective-permute-done.9
  173.7 1.3 collective-permute-start.11
  175.0 1.3 collective-permute-start.10
  176.3 4.2 %collective-permute-done.10 = f32[3,10,1]{2,1,0:T(8,128)S(1)} collective-permute-done((f32[3,10,1]{2,1,0:T(8,128)S(1)}, f32[3,10,1]{2,1,0:T(8,128)S(1)}, u32[]{:S(2)}, u32[]{:S(2)}) %collective-permute-start.10) | collective-permute-done | bytes 152 | tf_op jit(solution)/shard_map/ppermute | solution.py:19
  181.2 40.2 %psum.87 = f32[]{:T(128)} all-reduce(f32[]{:T(128)} %get-tuple-element.14), channel_id=1, replica_groups=mesh['row'=8,'col'=4] {'row','col'}, use_global_device_ids=true, to_apply=%region_15.0 | all-reduce | flops 1 | bytes 8 | tf_op jit(solution)/shard_map/psum | solution.py:97
  (49 shorter events, 11.0 us)
Async XLA Ops:
  0.6 52.6 %copy-start = (f32[16,64]{1,0:T(8,128)S(1)}, f32[16,64]{1,0:T(8,128)}, u32[]{:S(2)}) copy-start(f32[16,64]{1,0:T(8,128)} %param.9) | copy-start | bytes 12292
  1.4 60.5 %collective-permute-start = (f32[1,128]{1,0:T(1,128)S(1)}, f32[1,128]{1,0:T(1,128)S(1)}, u32[]{:S(2)}, u32[]{:S(2)}) collective-permute-start(f32[1,128]{1,0:T(1,128)S(1)} %get-tuple-element.37), channel_id=1, source_target_pairs={{4,0},{8,4},{12,8},{16,12},{20,16},{24,20},{28,24},{5,1},{9,5},{13... | collective-permute-start | bytes 1544 | tf_op jit(solution)/shard_map/ppermute | solution.py:19
  2.7 59.2 %collective-permute-start.1 = (f32[1,128]{1,0:T(1,128)S(1)}, f32[1,128]{1,0:T(1,128)S(1)}, u32[]{:S(2)}, u32[]{:S(2)}) collective-permute-start(f32[1,128]{1,0:T(1,128)S(1)} %get-tuple-element.36), channel_id=1, source_target_pairs={{0,4},{4,8},{8,12},{12,16},{16,20},{20,24},{24,28},{1,5},{5,9},{9,... | collective-permute-start | bytes 1544 | tf_op jit(solution)/shard_map/ppermute | solution.py:18
  9.5 1.1 copy-start.1
  9.5 1.1 copy-start.2
  53.4 0.7 copy-start.5
  61.3 0.7 copy-start.4
  62.0 5.3 %copy-start.3 = (s32[3,8,128]{2,1,0:T(8,128)S(1)}, s32[3,8,128]{2,1,0:T(8,128)}, u32[]{:S(2)}) copy-start(s32[3,8,128]{2,1,0:T(8,128)} %param.7) | copy-start | bytes 36868
  62.1 4.3 %collective-permute-start.2 = (f32[10,1]{1,0:T(8,128)S(1)}, f32[10,1]{1,0:T(8,128)S(1)}, u32[]{:S(2)}, u32[]{:S(2)}) collective-permute-start(f32[10,1]{1,0:T(8,128)S(1)} %get-tuple-element.35), channel_id=1, source_target_pairs={{1,0},{2,1},{3,2},{5,4},{6,5},{7,6},{9,8},{10,9},{11,10},{13,12},{... | collective-permute-start | bytes 128 | tf_op jit(solution)/shard_map/ppermute | solution.py:19
  63.4 3.8 %collective-permute-start.3 = (f32[10,1]{1,0:T(8,128)S(1)}, f32[10,1]{1,0:T(8,128)S(1)}, u32[]{:S(2)}, u32[]{:S(2)}) collective-permute-start(f32[10,1]{1,0:T(8,128)S(1)} %get-tuple-element.34), channel_id=1, source_target_pairs={{0,1},{1,2},{2,3},{4,5},{5,6},{6,7},{8,9},{9,10},{10,11},{12,13},{... | collective-permute-start | bytes 128 | tf_op jit(solution)/shard_map/ppermute | solution.py:18
  67.4 6.1 %collective-permute-start.4 = (f32[3,1,128]{2,1,0:T(1,128)S(1)}, f32[3,1,128]{2,1,0:T(1,128)S(1)}, u32[]{:S(2)}, u32[]{:S(2)}) collective-permute-start(f32[3,1,128]{2,1,0:T(1,128)S(1)} %get-tuple-element.33), channel_id=1, source_target_pairs={{4,0},{8,4},{12,8},{16,12},{20,16},{24,20},{28,24},{5,1},{9,5},{13... | collective-permute-start | bytes 4616 | tf_op jit(solution)/shard_map/ppermute | solution.py:19
  68.7 6.1 %collective-permute-start.5 = (f32[3,1,128]{2,1,0:T(1,128)S(1)}, f32[3,1,128]{2,1,0:T(1,128)S(1)}, u32[]{:S(2)}, u32[]{:S(2)}) collective-permute-start(f32[3,1,128]{2,1,0:T(1,128)S(1)} %get-tuple-element.32), channel_id=1, source_target_pairs={{0,4},{4,8},{8,12},{12,16},{16,20},{20,24},{24,28},{1,5},{5,9},{9,... | collective-permute-start | bytes 4616 | tf_op jit(solution)/shard_map/ppermute | solution.py:18
  74.9 4.3 %collective-permute-start.7 = (f32[3,10,1]{2,1,0:T(8,128)S(1)}, f32[3,10,1]{2,1,0:T(8,128)S(1)}, u32[]{:S(2)}, u32[]{:S(2)}) collective-permute-start(f32[3,10,1]{2,1,0:T(8,128)S(1)} %get-tuple-element.29), channel_id=1, source_target_pairs={{0,1},{1,2},{2,3},{4,5},{5,6},{6,7},{8,9},{9,10},{10,11},{12,13},{... | collective-permute-start | bytes 368 | tf_op jit(solution)/shard_map/ppermute | solution.py:18
  77.2 6.0 %collective-permute-start.6 = (f32[3,10,1]{2,1,0:T(8,128)S(1)}, f32[3,10,1]{2,1,0:T(8,128)S(1)}, u32[]{:S(2)}, u32[]{:S(2)}) collective-permute-start(f32[3,10,1]{2,1,0:T(8,128)S(1)} %get-tuple-element.28), channel_id=1, source_target_pairs={{1,0},{2,1},{3,2},{5,4},{6,5},{7,6},{9,8},{10,9},{11,10},{13,12},{... | collective-permute-start | bytes 368 | tf_op jit(solution)/shard_map/ppermute | solution.py:19
  166.5 5.9 %collective-permute-start.8 = (f32[3,1,128]{2,1,0:T(1,128)S(1)}, f32[3,1,128]{2,1,0:T(1,128)S(1)}, u32[]{:S(2)}, u32[]{:S(2)}) collective-permute-start(f32[3,1,128]{2,1,0:T(1,128)S(1)} %get-tuple-element.31), channel_id=1, source_target_pairs={{4,0},{8,4},{12,8},{16,12},{20,16},{24,20},{28,24},{5,1},{9,5},{13... | collective-permute-start | bytes 4616 | tf_op jit(solution)/shard_map/ppermute | solution.py:19
  167.8 5.8 %collective-permute-start.9 = (f32[3,1,128]{2,1,0:T(1,128)S(1)}, f32[3,1,128]{2,1,0:T(1,128)S(1)}, u32[]{:S(2)}, u32[]{:S(2)}) collective-permute-start(f32[3,1,128]{2,1,0:T(1,128)S(1)} %get-tuple-element.30), channel_id=1, source_target_pairs={{0,4},{4,8},{8,12},{12,16},{16,20},{20,24},{24,28},{1,5},{5,9},{9,... | collective-permute-start | bytes 4616 | tf_op jit(solution)/shard_map/ppermute | solution.py:18
  173.7 2.6 %collective-permute-start.11 = (f32[3,10,1]{2,1,0:T(8,128)S(1)}, f32[3,10,1]{2,1,0:T(8,128)S(1)}, u32[]{:S(2)}, u32[]{:S(2)}) collective-permute-start(f32[3,10,1]{2,1,0:T(8,128)S(1)} %get-tuple-element.27), channel_id=1, source_target_pairs={{0,1},{1,2},{2,3},{4,5},{5,6},{6,7},{8,9},{9,10},{10,11},{12,13},{... | collective-permute-start | bytes 368 | tf_op jit(solution)/shard_map/ppermute | solution.py:18
  175.0 5.5 %collective-permute-start.10 = (f32[3,10,1]{2,1,0:T(8,128)S(1)}, f32[3,10,1]{2,1,0:T(8,128)S(1)}, u32[]{:S(2)}, u32[]{:S(2)}) collective-permute-start(f32[3,10,1]{2,1,0:T(8,128)S(1)} %get-tuple-element.26), channel_id=1, source_target_pairs={{1,0},{2,1},{3,2},{5,4},{6,5},{7,6},{9,8},{10,9},{11,10},{13,12},{... | collective-permute-start | bytes 368 | tf_op jit(solution)/shard_map/ppermute | solution.py:19
